TPU v7x, 8 devices: a whole 2x2x1 slice. The times are simulated.
8 devices in a mesh: data: 1 (over z), tp: 8 (over y, x, core).
Axes of the slice: x: 2, y: 2, z: 1, core: 2. Of those that a mesh axis runs over, the one named last changes fastest.
Arguments:
- attn_ctx: bfloat16 [512, 12288], P('data', 'tp')
- w_attn_out: bfloat16 [12288, 12288], P('tp')
- mlp_act: bfloat16 [512, 49152], P('data', 'tp')
- w_mlp_down: bfloat16 [49152, 12288], P('tp')
Outputs:
- output: bfloat16 [512, 12288], P('data')
All inputs are finite; a program needn't handle non-finite values.
Results may differ from a plain program's by a relative error of at most 0.0116369.
Values are sent between devices in bfloat16 or wider.
A program may use at most 1 GiB of HBM per device.

v0:
```python
import jax
import jax.numpy as jnp
from jax import lax
from jax.sharding import PartitionSpec as P


def solution(mesh):
    def device_step(ctx_block, w_out_block, act_block, w_down_block):
        part_sum = jnp.dot(ctx_block, w_out_block, preferred_element_type=jnp.float32)
        part_sum = part_sum + jnp.dot(act_block, w_down_block, preferred_element_type=jnp.float32)
        row_sum = lax.psum_scatter(part_sum.astype(jnp.bfloat16), "tp", scatter_dimension=0, tiled=True)
        return lax.all_gather(row_sum, "tp", axis=0, tiled=True)

    return jax.shard_map(
        device_step,
        mesh=mesh,
        in_specs=(P("data", "tp"), P("tp", None), P("data", "tp"), P("tp", None)),
        out_specs=P("data", None),
        check_vma=False,
    )
```

profile of v0, /device:TPU:0, one launch (start us, length us, event | category | flops | bytes accessed | tf_op | source)
XLA Modules:
  0.0 297.4 jit_solution(5266341656476844234)
XLA Ops:
  6.5 0.0 copy-start
  6.5 0.0 reduce-scatter.2.cloned.1.call-start
  6.5 1.4 copy-done
  7.9 28.8 %fusion = f32[512,12288]{1,0:T(8,128)} fusion(bf16[512,1536]{1,0:T(8,128)(2,1)S(1)} %copy-done, bf16[1536,12288]{1,0:T(8,128)(2,1)} %param.5), kind=kOutput, calls=%fused_computation.1 | convolution fusion | flops 19327352832 | bytes 64487424 | tf_op jit(solution)/shard_map/dot_general | solution.py:9
  36.8 0.0 copy-start.1
  36.8 89.5 %add_convert_fusion = bf16[512,12288]{1,0:T(8,128)(2,1)} fusion(f32[512,12288]{1,0:T(8,128)} %fusion, bf16[512,6144]{1,0:T(8,128)(2,1)} %param.6, bf16[6144,12288]{1,0:T(8,128)(2,1)} %param.7), kind=kOutput, calls=%fused_computation | convolution fusion | flops 77321994240 | bytes 195035136 | tf_op jit(solution)/shard_map/dot_general | solution.py:10
  126.3 0.0 reduce-scatter.2.cloned.1.call-update
  126.4 0.0 all-gather.2.cloned.1.call-start
  126.4 85.4 %reduce-scatter.2.cloned.1.call-done = bf16[64,12288]{1,0:T(8,128)(2,1)} async-done(((bf16[512,12288]{1,0:T(8,128)(2,1)}), bf16[64,12288]{1,0:T(8,128)(2,1)}) %reduce-scatter.2.cloned.1.call-update) | async-done | bytes 1572880 | tf_op jit(solution)/shard_map/reduce_scatter | solution.py:11
  211.8 0.0 all-gather.2.cloned.1.call-update
  211.8 68.1 %all-gather.2.cloned.1.call-done = bf16[512,12288]{1,0:T(8,128)(2,1)} async-done(((bf16[64,12288]{1,0:T(8,128)(2,1)}), bf16[512,12288]{1,0:T(8,128)(2,1)}) %all-gather.2.cloned.1.call-update) | async-done | bytes 12582928 | tf_op jit(solution)/shard_map/all_gather | solution.py:12
  279.9 10.6 %copy.6 = bf16[512,12288]{1,0:T(8,128)(2,1)} copy(bf16[512,12288]{1,0:T(8,128)(2,1)} %all-gather.2.cloned.1.call-done) | data formatting | bytes 25165824
  290.6 0.0 copy-done.1
Async XLA Ops:
  6.5 1.4 copy-start
  6.5 205.3 %reduce-scatter.2.cloned.1.call-start = ((), (), s32[]{:S(2)}) async-start(), calls=%async_computation.1 | async-start | bytes 14155776 | tf_op jit(solution)/shard_map/reduce_scatter | solution.py:11
  36.8 253.8 %copy-start.1 = (bf16[512,1536]{1,0:T(8,128)(2,1)S(1)}, bf16[512,1536]{1,0:T(8,128)(2,1)}, u32[]{:S(2)}) copy-start(bf16[512,1536]{1,0:T(8,128)(2,1)} %param.4) | copy-start | bytes 4718596
  126.4 153.6 %all-gather.2.cloned.1.call-start = ((), (), s32[]{:S(2)}) async-start(), calls=%async_computation.2 | async-start | bytes 14155776 | tf_op jit(solution)/shard_map/all_gather | solution.py:12
Sparse Core Ops, SparseCore 0:
  126.5 85.2 reduce-scatter.1
  213.6 66.2 all-gather.1
where the time goes:
time: 298 us; the launch traced here: 297 us
  waiting for transfers between devices  154 us (52%)
  matrix products  118 us (40%)
  between operations  13.4 us (4%)
  local copies, waits for them, and re-layouts  12.1 us (4%)
    dot_general x1, matrix products, device_step(): jnp.dot(act_block, w_down_block, preferred_element_type=jnp.float32)  89.5 us
    reduce_scatter x1, waiting for transfers between devices, device_step(): lax.psum_scatter(part_sum.astype(jnp.bfloat16), 'tp', scatter_dimension=0...  85.4 us
    all_gather x1, waiting for transfers between devices, device_step(): return lax.all_gather(row_sum, 'tp', axis=0, tiled=True)  68.1 us
    dot_general x1, matrix products, device_step(): jnp.dot(ctx_block, w_out_block, preferred_element_type=jnp.float32)  28.8 us
    unnamed x5, local copies, waits for them, and re-layouts  12.1 us
  transfers between devices with their start and end apart: 2, of which 2 were waited for; matrix products, arithmetic and copies ran while one was open for 0% of the time, Pallas kernels for 0%

commit v1 on v0

v1 whole, which is shorter than its diff:
```python
import functools

import jax
import jax.numpy as jnp
from jax import lax
from jax.experimental import pallas as pl
from jax.experimental.pallas import tpu as pltpu
from jax.sharding import PartitionSpec as P

MESH = pl.DeviceIdType.MESH
BF16 = jnp.bfloat16
F32 = jnp.float32

W = 512
D1, D2, D3, D4, D5 = 1, 3, 4, 5, 7
SLOTS = 4


def kernel(n_chunks, ctx_ref, wo_ref, act_ref, wd_ref, y_ref, x_v, w_v, recv0, recv1, recv2, send0, send1, send2, keep0, keep1, keep2, x_sem, w_sem, s_sem, r_sem):
    me = lax.axis_index("tp")
    core = lax.rem(me, 2)
    cx = lax.rem(me // 2, 2)
    cy = me // 4
    p_core = me + 1 - 2 * core
    p_x = me + 2 - 4 * cx
    p_y = me + 4 - 8 * cy
    ka = ctx_ref.shape[1]
    km = act_ref.shape[1]

    def half_rows(c):
        base = 256 * c
        h1 = [
            base + 64 * (1 - cx) + 32 * (1 - cy),
            base + 64 * (1 - cx) + 32 * cy,
            base + 64 * cx + 32 * (1 - cy),
            base + 64 * cx + 32 * cy,
        ]
        base = base + 128
        h2 = [
            base + 64 * (1 - cy) + 32 * (1 - cx),
            base + 64 * (1 - cy) + 32 * cx,
            base + 64 * cy + 32 * (1 - cx),
            base + 64 * cy + 32 * cx,
        ]
        return h1 + h2

    rows = half_rows(1 - core) + half_rows(core)
    base1 = 256 * core + 64 * cx
    base2 = 256 * core + 128 + 64 * cy
    own1 = base1 + 32 * cy
    own2 = base2 + 32 * cx

    def w_copies(c, slot):
        cols = pl.ds(pl.multiple_of(c * W, W), W)
        out = []
        for j in range(ka // 1536):
            out.append(pltpu.make_async_copy(wo_ref.at[pl.ds(j * 1536, 1536), cols], w_v.at[slot, pl.ds(j * 1536, 1536)], w_sem.at[slot, len(out)]))
        for j in range(km // 1536):
            out.append(pltpu.make_async_copy(wd_ref.at[pl.ds(j * 1536, 1536), cols], w_v.at[slot, pl.ds(ka + j * 1536, 1536)], w_sem.at[slot, len(out)]))
        return out

    for cp in w_copies(0, 0):
        cp.start()
    for b, r in enumerate(rows):
        r = pl.multiple_of(r, 32)
        pltpu.make_async_copy(ctx_ref.at[pl.ds(r, 32)], x_v.at[pl.ds(32 * b, 32), pl.ds(0, ka)], x_sem.at[0]).start()
        pltpu.make_async_copy(act_ref.at[pl.ds(r, 32)], x_v.at[pl.ds(32 * b, 32), pl.ds(ka, km)], x_sem.at[1]).start()

    barrier = pltpu.get_barrier_semaphore()
    for p in (p_core, p_x, p_y):
        pl.semaphore_signal(barrier, inc=1, device_id={"tp": p}, device_id_type=MESH)
    pl.semaphore_wait(barrier, 3)

    def remote(src, dst, k, c, to):
        return pltpu.make_async_remote_copy(
            src_ref=src, dst_ref=dst, send_sem=s_sem.at[k, lax.rem(c, SLOTS)], recv_sem=r_sem.at[k, c], device_id={"tp": to}, device_id_type=MESH
        )

    def y_at(r, n, c):
        return y_ref.at[pl.ds(pl.multiple_of(r, 32), n), pl.ds(pl.multiple_of(c * W, W), W)]

    def p0(c):
        return [remote(send0.at[lax.rem(c, 2)], recv0.at[c], 0, c, p_core)]

    def p1(c):
        s = lax.rem(c, SLOTS)
        return [remote(send1.at[s, 0], recv1.at[c, 0], 1, c, p_x), remote(send1.at[s, 1], recv1.at[c, 1], 2, c, p_y)]

    def p2(c):
        s = lax.rem(c, SLOTS)
        return [remote(send2.at[s, 0], recv2.at[c, 0], 3, c, p_y), remote(send2.at[s, 1], recv2.at[c, 1], 4, c, p_x)]

    def p3(c):
        return [remote(y_at(own1, 32, c), y_at(own1, 32, c), 5, c, p_y), remote(y_at(own2, 32, c), y_at(own2, 32, c), 6, c, p_x)]

    def p4(c):
        return [remote(y_at(base1, 64, c), y_at(base1, 64, c), 7, c, p_x), remote(y_at(base2, 64, c), y_at(base2, 64, c), 8, c, p_y)]

    def p5(c):
        half = 256 * core
        return [remote(y_at(half, 256, c), y_at(half, 256, c), 9, c, p_core)]

    def guard(cond, fn):
        if isinstance(cond, bool):
            if cond:
                fn()
        else:
            pl.when(cond)(fn)

    def drain(make, c):
        def fn():
            for d in make(c - SLOTS):
                d.wait_send()

        guard(c >= SLOTS, fn)

    def start(make, c):
        drain(make, c)
        for d in make(c):
            d.start()

    def stage0(c):
        for d in p0(c):
            d.wait_recv()
        k = lax.rem(c, SLOTS)
        drain(p1, c)
        for h in range(2):
            o = 128 * h
            send1[k, h] = (keep0[lax.rem(c, 2), o : o + 64] + recv0[c, o : o + 64].astype(F32)).astype(BF16)
            keep1[k, h] = keep0[lax.rem(c, 2), o + 64 : o + 128] + recv0[c, o + 64 : o + 128].astype(F32)
        for d in p1(c):
            d.start()

    def stage1(c):
        for d in p1(c):
            d.wait_recv()
        k = lax.rem(c, SLOTS)
        drain(p2, c)
        for h in range(2):
            send2[k, h] = (keep1[k, h, 0:32] + recv1[c, h, 0:32].astype(F32)).astype(BF16)
            keep2[k, h] = keep1[k, h, 32:64] + recv1[c, h, 32:64].astype(F32)
        for d in p2(c):
            d.start()

    def stage2(c):
        for d in p2(c):
            d.wait_recv()
        k = lax.rem(c, SLOTS)
        cols = pl.ds(pl.multiple_of(c * W, W), W)
        for h, r in enumerate((own1, own2)):
            y_ref[pl.ds(pl.multiple_of(r, 32), 32), cols] = (keep2[k, h] + recv2[c, h].astype(F32)).astype(BF16)
        start(p3, c)

    def stage3(c):
        for d in p3(c):
            d.wait_recv()
        start(p4, c)

    def stage4(c):
        for d in p4(c):
            d.wait_recv()
        start(p5, c)

    stages = ((D5, stage4), (D4, stage3), (D3, stage2), (D2, stage1), (D1, stage0))

    pltpu.make_async_copy(ctx_ref, x_v.at[:, pl.ds(0, ka)], x_sem.at[0]).wait()
    pltpu.make_async_copy(act_ref, x_v.at[:, pl.ds(ka, km)], x_sem.at[1]).wait()

    def step(i, carry):
        slot = lax.rem(i, 2)
        for cp in w_copies(i, slot):
            cp.wait()

        @pl.when(i + 1 < n_chunks)
        def _():
            for cp in w_copies(i + 1, 1 - slot):
                cp.start()

        @pl.when(i >= 2)
        def _():
            for d in p0(i - 2):
                d.wait_send()

        part = jnp.dot(x_v[...], w_v[slot], preferred_element_type=F32)
        send0[slot] = part[0:256].astype(BF16)
        keep0[slot] = part[256:512]
        for d in p0(i):
            d.start()
        for delay, fn in stages:
            pl.when(i >= delay)(functools.partial(fn, i - delay))
        return carry

    lax.fori_loop(0, n_chunks, step, 0)
    for i in range(n_chunks, n_chunks + D5):
        for delay, fn in stages:
            if 0 <= i - delay < n_chunks:
                fn(i - delay)
    for d in p0(n_chunks - 2) + p0(n_chunks - 1):
        d.wait_send()
    for c in range(n_chunks - SLOTS, n_chunks):
        for make in (p1, p2, p3, p4, p5):
            for d in make(c):
                d.wait_send()
    for c in range(n_chunks):
        for d in p5(c):
            d.wait_recv()


def solution(mesh):
    def device_step(ctx, w_out, act, w_down):
        rows, ka = ctx.shape
        km, cols = w_down.shape
        n = cols // W
        any_ = pl.BlockSpec(memory_space=pl.ANY)
        return pl.pallas_call(
            functools.partial(kernel, n),
            out_shape=jax.ShapeDtypeStruct((rows, cols), BF16),
            in_specs=[any_] * 4,
            out_specs=pl.BlockSpec(memory_space=pltpu.VMEM),
            scratch_shapes=[
                pltpu.VMEM((rows, ka + km), BF16),
                pltpu.VMEM((2, ka + km, W), BF16),
                pltpu.VMEM((n, 256, W), BF16),
                pltpu.VMEM((n, 2, 64, W), BF16),
                pltpu.VMEM((n, 2, 32, W), BF16),
                pltpu.VMEM((2, 256, W), BF16),
                pltpu.VMEM((SLOTS, 2, 64, W), BF16),
                pltpu.VMEM((SLOTS, 2, 32, W), BF16),
                pltpu.VMEM((2, 256, W), F32),
                pltpu.VMEM((SLOTS, 2, 64, W), F32),
                pltpu.VMEM((SLOTS, 2, 32, W), F32),
                pltpu.SemaphoreType.DMA((2,)),
                pltpu.SemaphoreType.DMA((2, (ka + km) // 1536)),
                pltpu.SemaphoreType.DMA((10, SLOTS)),
                pltpu.SemaphoreType.DMA((10, n)),
            ],
            compiler_params=pltpu.CompilerParams(collective_id=0, has_side_effects=True, vmem_limit_bytes=60 * 1024 * 1024),
            cost_estimate=pl.CostEstimate(flops=2 * rows * (ka + km) * cols, bytes_accessed=2 * (ka + km) * cols, transcendentals=0),
        )(ctx, w_out, act, w_down)

    return jax.shard_map(
        device_step,
        mesh=mesh,
        in_specs=(P("data", "tp"), P("tp", None), P("data", "tp"), P("tp", None)),
        out_specs=P("data", None),
        check_vma=False,
    )
```

time: 298 us -> 157 us (0.53)
  waiting for transfers between devices: 154 us -> 0 us
  Pallas kernels: 0 us -> 146 us
  matrix products: 118 us -> 0 us
  between operations: 13.4 us -> 0.01 us
    pallas_call x0 -> x1, Pallas kernels: none -> 146 us  [device_step(): pl.pallas_call(functools.partial(kernel, n), out_shape=jax.ShapeDtypeStru...]
    dot_general x2 -> x0, matrix products: 118 us -> none  [the longest x1 89.5 us: device_step(): jnp.dot(act_block, w_down_block, preferred_element_type=jnp.float32)]
    reduce_scatter x1 -> x0, waiting for transfers between devices: 85.4 us -> none  [device_step(): lax.psum_scatter(part_sum.astype(jnp.bfloat16), 'tp', scatter_dimension=0...]
    all_gather x1 -> x0, waiting for transfers between devices: 68.1 us -> none  [device_step(): return lax.all_gather(row_sum, 'tp', axis=0, tiled=True)]
    unnamed x5 -> x1, local copies, waits for them, and re-layouts: 12.1 us -> 10.7 us
  transfers between devices with their start and end apart: 2 -> 0, of which waited for: 2 -> 0; matrix products, arithmetic and copies ran while one was open for 0% -> 0% of each run, Pallas kernels for 0% -> 0%
where the time goes in v1:
time: 157 us; the launch traced here: 156 us
  Pallas kernels  146 us (93%)
  local copies, waits for them, and re-layouts  10.7 us (7%)
    pallas_call x1, Pallas kernels, device_step(): pl.pallas_call(functools.partial(kernel, n), out_shape=jax.ShapeDtypeStru...  146 us
    unnamed x1, local copies, waits for them, and re-layouts  10.7 us

profile of v1, /device:TPU:0, one launch (start us, length us, event | category | flops | bytes accessed | tf_op | source)
XLA Modules:
  0.0 156.5 jit_solution(11783494457905209331)
XLA Ops:
  0.0 145.8 %shard_map.46 = bf16[512,12288]{1,0:T(8,128)(2,1)} custom-call(bf16[512,1536]{1,0:T(8,128)(2,1)} %ctx_ref.1, bf16[1536,12288]{1,0:T(8,128)(2,1)} %wo_ref.1, bf16[512,6144]{1,0:T(8,128)(2,1)} %act_ref.1, bf16[6144,12288]{1,0:T(8,128)(2,1)} %wd_ref.1), custom_call_target="tpu_custom_call" | custom-call | flops 96636764160 | bytes 188743680 | tf_op jit(solution)/shard_map/pallas_call | solution.py:215
  145.8 10.7 %copy.6 = bf16[512,12288]{1,0:T(8,128)(2,1)} copy(bf16[512,12288]{1,0:T(8,128)(2,1)} %shard_map.46) | data formatting | bytes 25165824

commit v2 on v1

--- a/solution.py
+++ b/solution.py
@@ -14,6 +14,7 @@
 W = 512
 D1, D2, D3, D4, D5 = 1, 3, 4, 5, 7
 SLOTS = 4
+VMEM_LIMIT = 44 * 1024 * 1024
 
 
 def kernel(n_chunks, ctx_ref, wo_ref, act_ref, wd_ref, y_ref, x_v, w_v, recv0, recv1, recv2, send0, send1, send2, keep0, keep1, keep2, x_sem, w_sem, s_sem, r_sem):
@@ -206,15 +207,27 @@
             d.wait_recv()
 
 
+STORES = 8
+
+
+def store(y_ref, o_ref, sem):
+    n = y_ref.shape[0] // STORES
+    copies = [pltpu.make_async_copy(y_ref.at[pl.ds(j * n, n)], o_ref.at[pl.ds(j * n, n)], sem.at[j]) for j in range(STORES)]
+    for cp in copies:
+        cp.start()
+    for cp in copies:
+        cp.wait()
+
+
 def solution(mesh):
     def device_step(ctx, w_out, act, w_down):
         rows, ka = ctx.shape
         km, cols = w_down.shape
         n = cols // W
         any_ = pl.BlockSpec(memory_space=pl.ANY)
-        return pl.pallas_call(
+        y = pl.pallas_call(
             functools.partial(kernel, n),
-            out_shape=jax.ShapeDtypeStruct((rows, cols), BF16),
+            out_shape=pltpu.VMEM((rows, cols), BF16),
             in_specs=[any_] * 4,
             out_specs=pl.BlockSpec(memory_space=pltpu.VMEM),
             scratch_shapes=[
@@ -234,9 +247,18 @@
                 pltpu.SemaphoreType.DMA((10, SLOTS)),
                 pltpu.SemaphoreType.DMA((10, n)),
             ],
-            compiler_params=pltpu.CompilerParams(collective_id=0, has_side_effects=True, vmem_limit_bytes=60 * 1024 * 1024),
+            compiler_params=pltpu.CompilerParams(collective_id=0, has_side_effects=True, vmem_limit_bytes=VMEM_LIMIT),
             cost_estimate=pl.CostEstimate(flops=2 * rows * (ka + km) * cols, bytes_accessed=2 * (ka + km) * cols, transcendentals=0),
         )(ctx, w_out, act, w_down)
+        return pl.pallas_call(
+            store,
+            out_shape=jax.ShapeDtypeStruct((rows, cols), BF16),
+            in_specs=[pl.BlockSpec(memory_space=pltpu.VMEM)],
+            out_specs=pl.BlockSpec(memory_space=pl.ANY),
+            scratch_shapes=[pltpu.SemaphoreType.DMA((STORES,))],
+            compiler_params=pltpu.CompilerParams(vmem_limit_bytes=1024 * 1024),
+            cost_estimate=pl.CostEstimate(flops=0, bytes_accessed=2 * rows * cols, transcendentals=0),
+        )(y)
 
     return jax.shard_map(
         device_step,

time: 157 us -> 146 us (0.930)
  local copies, waits for them, and re-layouts: 10.7 us -> 0 us
    unnamed x1 -> x0, local copies, waits for them, and re-layouts: 10.7 us -> none
    pallas_call x1 -> x2, Pallas kernels: 146 us -> 146 us  [the longest x1 141 us: device_step(): pl.pallas_call(functools.partial(kernel, n), out_shape=pltpu.VMEM((rows,...]
where the time goes in v2:
time: 146 us
  Pallas kernels  146 us (100%)
    pallas_call x1, Pallas kernels, device_step(): pl.pallas_call(functools.partial(kernel, n), out_shape=pltpu.VMEM((rows,...  141 us
    pallas_call x1, Pallas kernels, device_step(): pl.pallas_call(store, out_shape=jax.ShapeDtypeStruct((rows, cols), BF16),...  4.66 us

profile of v2, /device:TPU:0, one launch (start us, length us, event | category | flops | bytes accessed | tf_op | source)
XLA Modules:
  0.0 146.0 jit_solution(4129024471751356317)
XLA Ops:
  0.0 141.3 %shard_map.46.y_ref = bf16[512,12288]{1,0:T(8,128)(2,1)S(1)} custom-call(bf16[512,1536]{1,0:T(8,128)(2,1)} %ctx_ref.1, bf16[1536,12288]{1,0:T(8,128)(2,1)} %wo_ref.1, bf16[512,6144]{1,0:T(8,128)(2,1)} %act_ref.1, bf16[6144,12288]{1,0:T(8,128)(2,1)} %wd_ref.1), custom_call_target="tpu_custom_call" | custom-call | flops 96636764160 | bytes 188743680 | tf_op jit(solution)/shard_map/pallas_call | solution.py:228
  141.3 4.7 %shard_map.47 = bf16[512,12288]{1,0:T(8,128)(2,1)} custom-call(bf16[512,12288]{1,0:T(8,128)(2,1)S(1)} %shard_map.46.y_ref), custom_call_target="tpu_custom_call" | custom-call | bytes 12582912 | tf_op jit(solution)/shard_map/pallas_call | solution.py:253

commit v3 on v2

--- a/solution.py
+++ b/solution.py
@@ -12,9 +12,13 @@
 F32 = jnp.float32
 
 W = 512
-D1, D2, D3, D4, D5 = 1, 3, 4, 5, 7
+PARTS = 1
+LAG = (1, 3, 5, 6, 8)
+HEAD = 1
 SLOTS = 4
+STORES = 8
 VMEM_LIMIT = 44 * 1024 * 1024
+DRAIN = ((4, 8), (2, 5), (0, 1), (1, 3), (4, 7), (3, 6), (2, 4), (1, 2), (3, 5), (1, 1), (2, 3), (4, 6), (3, 4), (2, 2), (4, 5), (2, 1), (3, 3), (4, 4), (3, 2), (3, 1), (4, 3), (4, 2), (4, 1))
 
 
 def kernel(n_chunks, ctx_ref, wo_ref, act_ref, wd_ref, y_ref, x_v, w_v, recv0, recv1, recv2, send0, send1, send2, keep0, keep1, keep2, x_sem, w_sem, s_sem, r_sem):
@@ -60,17 +64,23 @@
             out.append(pltpu.make_async_copy(wd_ref.at[pl.ds(j * 1536, 1536), cols], w_v.at[slot, pl.ds(ka + j * 1536, 1536)], w_sem.at[slot, len(out)]))
         return out
 
-    for cp in w_copies(0, 0):
-        cp.start()
-    for b, r in enumerate(rows):
-        r = pl.multiple_of(r, 32)
-        pltpu.make_async_copy(ctx_ref.at[pl.ds(r, 32)], x_v.at[pl.ds(32 * b, 32), pl.ds(0, ka)], x_sem.at[0]).start()
-        pltpu.make_async_copy(act_ref.at[pl.ds(r, 32)], x_v.at[pl.ds(32 * b, 32), pl.ds(ka, km)], x_sem.at[1]).start()
+    def x_copies(j):
+        out = []
+        for b, r in enumerate(rows):
+            r = pl.multiple_of(r, 32)
+            src = ctx_ref.at[pl.ds(r, 32), pl.ds(j * 1536, 1536)] if j * 1536 < ka else act_ref.at[pl.ds(r, 32), pl.ds(j * 1536 - ka, 1536)]
+            out.append(pltpu.make_async_copy(src, x_v.at[pl.ds(32 * b, 32), pl.ds(j * 1536, 1536)], x_sem.at[j]))
+        return out
 
     barrier = pltpu.get_barrier_semaphore()
     for p in (p_core, p_x, p_y):
         pl.semaphore_signal(barrier, inc=1, device_id={"tp": p}, device_id_type=MESH)
-    pl.semaphore_wait(barrier, 3)
+    n_slices = (ka + km) // 1536
+    first = w_copies(0, 0)
+    for j in range(n_slices):
+        first[j].start()
+        for cp in x_copies(j):
+            cp.start()
 
     def remote(src, dst, k, c, to):
         return pltpu.make_async_remote_copy(
@@ -162,40 +172,67 @@
             d.wait_recv()
         start(p5, c)
 
-    stages = ((D5, stage4), (D4, stage3), (D3, stage2), (D2, stage1), (D1, stage0))
-
-    pltpu.make_async_copy(ctx_ref, x_v.at[:, pl.ds(0, ka)], x_sem.at[0]).wait()
-    pltpu.make_async_copy(act_ref, x_v.at[:, pl.ds(ka, km)], x_sem.at[1]).wait()
-
-    def step(i, carry):
-        slot = lax.rem(i, 2)
+    stages = (stage0, stage1, stage2, stage3, stage4)
+    part_k = (ka + km) // PARTS
+
+    def serve(i, q, static):
+        for k in (4, 3, 2, 1, 0):
+            back, rem = divmod(LAG[k] + PARTS - 1 - q, PARTS)
+            if rem == 0:
+                guard(i >= back, functools.partial(stages[k], i - back))
+
+    def finish(i, slot, total):
+        send0[slot] = total[0:256].astype(BF16)
+        keep0[slot] = total[256:512]
+        for d in p0(i):
+            d.start()
+
+    total = None
+    for j in range(n_slices):
+        first[j].wait()
+        pltpu.make_async_copy(ctx_ref.at[:, pl.ds(0, 1536)], x_v.at[:, pl.ds(j * 1536, 1536)], x_sem.at[j]).wait()
+        if j == 0:
+            for cp in w_copies(1, 1):
+                cp.start()
+        piece = jnp.dot(x_v[:, j * 1536 : (j + 1) * 1536], w_v[0, j * 1536 : (j + 1) * 1536], preferred_element_type=F32)
+        total = piece if total is None else total + piece
+    pl.semaphore_wait(barrier, 3)
+    finish(0, 0, total)
+
+    def step(i, static):
+        slot = i % 2 if static else lax.rem(i, 2)
         for cp in w_copies(i, slot):
             cp.wait()
 
-        @pl.when(i + 1 < n_chunks)
-        def _():
+        def ahead():
             for cp in w_copies(i + 1, 1 - slot):
                 cp.start()
 
-        @pl.when(i >= 2)
-        def _():
+        guard(i + 1 < n_chunks, ahead)
+
+        def sent():
             for d in p0(i - 2):
                 d.wait_send()
 
-        part = jnp.dot(x_v[...], w_v[slot], preferred_element_type=F32)
-        send0[slot] = part[0:256].astype(BF16)
-        keep0[slot] = part[256:512]
-        for d in p0(i):
-            d.start()
-        for delay, fn in stages:
-            pl.when(i >= delay)(functools.partial(fn, i - delay))
+        guard(i >= 2, sent)
+        total = None
+        for q in range(PARTS):
+            piece = jnp.dot(x_v[:, q * part_k : (q + 1) * part_k], w_v[slot, q * part_k : (q + 1) * part_k], preferred_element_type=F32)
+            total = piece if total is None else total + piece
+            if q == PARTS - 1:
+                finish(i, slot, total)
+            serve(i, q, static)
+
+    for i in range(1, HEAD):
+        step(i, True)
+
+    def looped(i, carry):
+        step(i, False)
         return carry
 
-    lax.fori_loop(0, n_chunks, step, 0)
-    for i in range(n_chunks, n_chunks + D5):
-        for delay, fn in stages:
-            if 0 <= i - delay < n_chunks:
-                fn(i - delay)
+    lax.fori_loop(HEAD, n_chunks, looped, 0)
+    for k, back in DRAIN:
+        stages[k](n_chunks - back)
     for d in p0(n_chunks - 2) + p0(n_chunks - 1):
         d.wait_send()
     for c in range(n_chunks - SLOTS, n_chunks):
@@ -205,9 +242,6 @@
     for c in range(n_chunks):
         for d in p5(c):
             d.wait_recv()
-
-
-STORES = 8
 
 
 def store(y_ref, o_ref, sem):
@@ -242,7 +276,7 @@
                 pltpu.VMEM((2, 256, W), F32),
                 pltpu.VMEM((SLOTS, 2, 64, W), F32),
                 pltpu.VMEM((SLOTS, 2, 32, W), F32),
-                pltpu.SemaphoreType.DMA((2,)),
+                pltpu.SemaphoreType.DMA(((ka + km) // 1536,)),
                 pltpu.SemaphoreType.DMA((2, (ka + km) // 1536)),
                 pltpu.SemaphoreType.DMA((10, SLOTS)),
                 pltpu.SemaphoreType.DMA((10, n)),

time: 146 us -> 142 us (0.973)
  Pallas kernels: 146 us -> 142 us
    pallas_call x1, Pallas kernels: 141 us -> 137 us  [device_step(): pl.pallas_call(functools.partial(kernel, n), out_shape=pltpu.VMEM((rows,...]
where the time goes in v3:
time: 142 us
  Pallas kernels  142 us (100%)
    pallas_call x1, Pallas kernels, device_step(): pl.pallas_call(functools.partial(kernel, n), out_shape=pltpu.VMEM((rows,...  137 us
    pallas_call x1, Pallas kernels, device_step(): pl.pallas_call(store, out_shape=jax.ShapeDtypeStruct((rows, cols), BF16),...  4.66 us

profile of v3, /device:TPU:0, one launch (start us, length us, event | category | flops | bytes accessed | tf_op | source)
XLA Modules:
  0.0 142.0 jit_solution(5651824632716052584)
XLA Ops:
  0.0 137.3 %shard_map.46.y_ref = bf16[512,12288]{1,0:T(8,128)(2,1)S(1)} custom-call(bf16[512,1536]{1,0:T(8,128)(2,1)} %ctx_ref.1, bf16[1536,12288]{1,0:T(8,128)(2,1)} %wo_ref.1, bf16[512,6144]{1,0:T(8,128)(2,1)} %act_ref.1, bf16[6144,12288]{1,0:T(8,128)(2,1)} %wd_ref.1), custom_call_target="tpu_custom_call" | custom-call | flops 96636764160 | bytes 188743680 | tf_op jit(solution)/shard_map/pallas_call | solution.py:262
  137.3 4.7 %shard_map.47 = bf16[512,12288]{1,0:T(8,128)(2,1)} custom-call(bf16[512,12288]{1,0:T(8,128)(2,1)S(1)} %shard_map.46.y_ref), custom_call_target="tpu_custom_call" | custom-call | bytes 12582912 | tf_op jit(solution)/shard_map/pallas_call | solution.py:287

commit v4 on v3

--- a/solution.py
+++ b/solution.py
@@ -12,13 +12,15 @@
 F32 = jnp.float32
 
 W = 512
-PARTS = 1
-LAG = (1, 3, 5, 6, 8)
-HEAD = 1
+K = 256
+CUTS = (0, 5, 15, 26, 30)
+LAG = ((1, 1), (3, 1), (4, 1), (5, 0), (6, 0))
+HEAD = 6
+UNROLL = 2
 SLOTS = 4
 STORES = 8
-VMEM_LIMIT = 44 * 1024 * 1024
-DRAIN = ((4, 8), (2, 5), (0, 1), (1, 3), (4, 7), (3, 6), (2, 4), (1, 2), (3, 5), (1, 1), (2, 3), (4, 6), (3, 4), (2, 2), (4, 5), (2, 1), (3, 3), (4, 4), (3, 2), (3, 1), (4, 3), (4, 2), (4, 1))
+VMEM_LIMIT = 48 * 1024 * 1024
+DRAIN = ((1, 3), (4, 6), (3, 5), (2, 4), (0, 1), (1, 2), (2, 3), (4, 5), (3, 4), (1, 1), (2, 2), (3, 3), (4, 4), (2, 1), (3, 2), (4, 3), (3, 1), (4, 2), (4, 1))
 
 
 def kernel(n_chunks, ctx_ref, wo_ref, act_ref, wd_ref, y_ref, x_v, w_v, recv0, recv1, recv2, send0, send1, send2, keep0, keep1, keep2, x_sem, w_sem, s_sem, r_sem):
@@ -173,64 +175,77 @@
         start(p5, c)
 
     stages = (stage0, stage1, stage2, stage3, stage4)
-    part_k = (ka + km) // PARTS
-
-    def serve(i, q, static):
+
+    def serve(i, cut, static):
         for k in (4, 3, 2, 1, 0):
-            back, rem = divmod(LAG[k] + PARTS - 1 - q, PARTS)
-            if rem == 0:
-                guard(i >= back, functools.partial(stages[k], i - back))
-
-    def finish(i, slot, total):
+            back, at = LAG[k]
+            if at == cut and (not static or i >= back):
+                stages[k](i - back)
+
+    def finish(c, slot, total):
+        def sent():
+            for d in p0(c - 2):
+                d.wait_send()
+
+        guard(c >= 2, sent)
         send0[slot] = total[0:256].astype(BF16)
         keep0[slot] = total[256:512]
-        for d in p0(i):
+        for d in p0(c):
             d.start()
 
+    def ahead(i, slot):
+        def fn():
+            for cp in w_copies(i + 1, 1 - slot):
+                cp.start()
+
+        guard(i + 1 < n_chunks, fn)
+
+    def here(i, slot):
+        def fn():
+            for cp in w_copies(i, slot):
+                cp.wait()
+
+        guard(i < n_chunks, fn)
+
+    def chunk(i, slot, before, static):
+        total = None
+        for cut in range(4):
+            k0, k1 = CUTS[cut] * K, CUTS[cut + 1] * K
+            piece = jnp.dot(x_v[:, k0:k1], w_v[slot, k0:k1], preferred_element_type=F32)
+            total = piece if total is None else piece + total
+            if cut == 0:
+                ahead(i, slot)
+                if before is not None:
+                    finish(i - 1, 1 - slot, before)
+            if cut < 2:
+                serve(i, cut, static)
+            if cut == 2:
+                here(i + 1, 1 - slot)
+        return total
+
+    pl.semaphore_wait(barrier, 3)
     total = None
     for j in range(n_slices):
         first[j].wait()
         pltpu.make_async_copy(ctx_ref.at[:, pl.ds(0, 1536)], x_v.at[:, pl.ds(j * 1536, 1536)], x_sem.at[j]).wait()
         if j == 0:
-            for cp in w_copies(1, 1):
-                cp.start()
+            ahead(0, 0)
         piece = jnp.dot(x_v[:, j * 1536 : (j + 1) * 1536], w_v[0, j * 1536 : (j + 1) * 1536], preferred_element_type=F32)
-        total = piece if total is None else total + piece
-    pl.semaphore_wait(barrier, 3)
-    finish(0, 0, total)
-
-    def step(i, static):
-        slot = i % 2 if static else lax.rem(i, 2)
-        for cp in w_copies(i, slot):
-            cp.wait()
-
-        def ahead():
-            for cp in w_copies(i + 1, 1 - slot):
-                cp.start()
-
-        guard(i + 1 < n_chunks, ahead)
-
-        def sent():
-            for d in p0(i - 2):
-                d.wait_send()
-
-        guard(i >= 2, sent)
+        total = piece if total is None else piece + total
+        if j == n_slices - 2:
+            here(1, 1)
+    for i in range(1, HEAD):
+        total = chunk(i, i % 2, total, True)
+    finish(HEAD - 1, (HEAD - 1) % 2, total)
+
+    def looped(j, carry):
         total = None
-        for q in range(PARTS):
-            piece = jnp.dot(x_v[:, q * part_k : (q + 1) * part_k], w_v[slot, q * part_k : (q + 1) * part_k], preferred_element_type=F32)
-            total = piece if total is None else total + piece
-            if q == PARTS - 1:
-                finish(i, slot, total)
-            serve(i, q, static)
-
-    for i in range(1, HEAD):
-        step(i, True)
-
-    def looped(i, carry):
-        step(i, False)
+        for h in range(UNROLL):
+            total = chunk(HEAD + UNROLL * j + h, h % 2, total, False)
+        finish(HEAD + UNROLL * j + UNROLL - 1, 1, total)
         return carry
 
-    lax.fori_loop(HEAD, n_chunks, looped, 0)
+    lax.fori_loop(0, (n_chunks - HEAD) // UNROLL, looped, 0)
     for k, back in DRAIN:
         stages[k](n_chunks - back)
     for d in p0(n_chunks - 2) + p0(n_chunks - 1):

time: 142 us -> 144 us (1.014)
  Pallas kernels: 142 us -> 144 us
    pallas_call x1, Pallas kernels: 137 us -> 139 us  [device_step(): pl.pallas_call(functools.partial(kernel, n), out_shape=pltpu.VMEM((rows,...]
where the time goes in v4:
time: 144 us
  Pallas kernels  144 us (100%)
    pallas_call x1, Pallas kernels, device_step(): pl.pallas_call(functools.partial(kernel, n), out_shape=pltpu.VMEM((rows,...  139 us
    pallas_call x1, Pallas kernels, device_step(): pl.pallas_call(store, out_shape=jax.ShapeDtypeStruct((rows, cols), BF16),...  4.66 us

profile of v4, /device:TPU:0, one launch (start us, length us, event | category | flops | bytes accessed | tf_op | source)
XLA Modules:
  0.0 143.8 jit_solution(15751920369823687565)
XLA Ops:
  0.0 139.0 %shard_map.46.y_ref = bf16[512,12288]{1,0:T(8,128)(2,1)S(1)} custom-call(bf16[512,1536]{1,0:T(8,128)(2,1)} %ctx_ref.1, bf16[1536,12288]{1,0:T(8,128)(2,1)} %wo_ref.1, bf16[512,6144]{1,0:T(8,128)(2,1)} %act_ref.1, bf16[6144,12288]{1,0:T(8,128)(2,1)} %wd_ref.1), custom_call_target="tpu_custom_call" | custom-call | flops 96636764160 | bytes 188743680 | tf_op jit(solution)/shard_map/pallas_call | solution.py:277
  139.0 4.7 %shard_map.47 = bf16[512,12288]{1,0:T(8,128)(2,1)} custom-call(bf16[512,12288]{1,0:T(8,128)(2,1)S(1)} %shard_map.46.y_ref), custom_call_target="tpu_custom_call" | custom-call | bytes 12582912 | tf_op jit(solution)/shard_map/pallas_call | solution.py:302

commit v5 on v3

--- a/solution.py
+++ b/solution.py
@@ -13,15 +13,16 @@
 
 W = 512
 PARTS = 1
-LAG = (1, 3, 5, 6, 8)
+LAG = (1, 2, 3, 4, 5)
 HEAD = 1
 SLOTS = 4
+DELAY = 3840
 STORES = 8
 VMEM_LIMIT = 44 * 1024 * 1024
-DRAIN = ((4, 8), (2, 5), (0, 1), (1, 3), (4, 7), (3, 6), (2, 4), (1, 2), (3, 5), (1, 1), (2, 3), (4, 6), (3, 4), (2, 2), (4, 5), (2, 1), (3, 3), (4, 4), (3, 2), (3, 1), (4, 3), (4, 2), (4, 1))
-
-
-def kernel(n_chunks, ctx_ref, wo_ref, act_ref, wd_ref, y_ref, x_v, w_v, recv0, recv1, recv2, send0, send1, send2, keep0, keep1, keep2, x_sem, w_sem, s_sem, r_sem):
+DRAIN = ((4, 5), (3, 4), (0, 1), (2, 3), (1, 2), (4, 4), (1, 1), (3, 3), (2, 2), (2, 1), (4, 3), (3, 2), (3, 1), (4, 2), (4, 1))
+
+
+def kernel(n_chunks, ctx_ref, wo_ref, act_ref, wd_ref, y_ref, x_v, w_v, recv0, recv1, recv2, send0, send1, send2, keep0, keep1, keep2, wait_v, x_sem, w_sem, s_sem, r_sem):
     me = lax.axis_index("tp")
     core = lax.rem(me, 2)
     cx = lax.rem(me // 2, 2)
@@ -195,9 +196,13 @@
             for cp in w_copies(1, 1):
                 cp.start()
         piece = jnp.dot(x_v[:, j * 1536 : (j + 1) * 1536], w_v[0, j * 1536 : (j + 1) * 1536], preferred_element_type=F32)
-        total = piece if total is None else total + piece
+        total = piece if total is None else piece + total
     pl.semaphore_wait(barrier, 3)
     finish(0, 0, total)
+
+    @pl.when(core == 1)
+    def _():
+        wait_v[...] = jnp.dot(x_v[:, 0:DELAY], w_v[0, 0:DELAY], preferred_element_type=F32)
 
     def step(i, static):
         slot = i % 2 if static else lax.rem(i, 2)
@@ -218,7 +223,7 @@
         total = None
         for q in range(PARTS):
             piece = jnp.dot(x_v[:, q * part_k : (q + 1) * part_k], w_v[slot, q * part_k : (q + 1) * part_k], preferred_element_type=F32)
-            total = piece if total is None else total + piece
+            total = piece if total is None else piece + total
             if q == PARTS - 1:
                 finish(i, slot, total)
             serve(i, q, static)
@@ -276,6 +281,7 @@
                 pltpu.VMEM((2, 256, W), F32),
                 pltpu.VMEM((SLOTS, 2, 64, W), F32),
                 pltpu.VMEM((SLOTS, 2, 32, W), F32),
+                pltpu.VMEM((rows, W), F32),
                 pltpu.SemaphoreType.DMA(((ka + km) // 1536,)),
                 pltpu.SemaphoreType.DMA((2, (ka + km) // 1536)),
                 pltpu.SemaphoreType.DMA((10, SLOTS)),

time: 142 us -> 150 us (1.056)
  Pallas kernels: 142 us -> 150 us
    pallas_call x1, Pallas kernels: 137 us -> 145 us  [device_step(): pl.pallas_call(functools.partial(kernel, n), out_shape=pltpu.VMEM((rows,...]
where the time goes in v5:
time: 150 us
  Pallas kernels  150 us (100%)
    pallas_call x1, Pallas kernels, device_step(): pl.pallas_call(functools.partial(kernel, n), out_shape=pltpu.VMEM((rows,...  145 us
    pallas_call x1, Pallas kernels, device_step(): pl.pallas_call(store, out_shape=jax.ShapeDtypeStruct((rows, cols), BF16),...  4.66 us

profile of v5, /device:TPU:0, one launch (start us, length us, event | category | flops | bytes accessed | tf_op | source)
XLA Modules:
  0.0 150.0 jit_solution(12476027328118454944)
XLA Ops:
  0.0 145.4 %shard_map.46.y_ref = bf16[512,12288]{1,0:T(8,128)(2,1)S(1)} custom-call(bf16[512,1536]{1,0:T(8,128)(2,1)} %ctx_ref.1, bf16[1536,12288]{1,0:T(8,128)(2,1)} %wo_ref.1, bf16[512,6144]{1,0:T(8,128)(2,1)} %act_ref.1, bf16[6144,12288]{1,0:T(8,128)(2,1)} %wd_ref.1), custom_call_target="tpu_custom_call" | custom-call | flops 96636764160 | bytes 188743680 | tf_op jit(solution)/shard_map/pallas_call | solution.py:267
  145.4 4.7 %shard_map.47 = bf16[512,12288]{1,0:T(8,128)(2,1)} custom-call(bf16[512,12288]{1,0:T(8,128)(2,1)S(1)} %shard_map.46.y_ref), custom_call_target="tpu_custom_call" | custom-call | bytes 12582912 | tf_op jit(solution)/shard_map/pallas_call | solution.py:293

commit v6 on v3

--- a/solution.py
+++ b/solution.py
@@ -13,12 +13,13 @@
 
 W = 512
 PARTS = 1
-LAG = (1, 3, 5, 6, 8)
+LAG = (1, 3, 4, 5, 7)
+ORDER = (1, 2, 3, 0, 4)
 HEAD = 1
 SLOTS = 4
 STORES = 8
 VMEM_LIMIT = 44 * 1024 * 1024
-DRAIN = ((4, 8), (2, 5), (0, 1), (1, 3), (4, 7), (3, 6), (2, 4), (1, 2), (3, 5), (1, 1), (2, 3), (4, 6), (3, 4), (2, 2), (4, 5), (2, 1), (3, 3), (4, 4), (3, 2), (3, 1), (4, 3), (4, 2), (4, 1))
+DRAIN = ((4, 7), (0, 1), (1, 3), (2, 4), (3, 5), (4, 6), (1, 2), (1, 1), (2, 3), (3, 4), (4, 5), (2, 2), (2, 1), (3, 3), (4, 4), (3, 2), (3, 1), (4, 3), (4, 2), (4, 1))
 
 
 def kernel(n_chunks, ctx_ref, wo_ref, act_ref, wd_ref, y_ref, x_v, w_v, recv0, recv1, recv2, send0, send1, send2, keep0, keep1, keep2, x_sem, w_sem, s_sem, r_sem):
@@ -176,7 +177,7 @@
     part_k = (ka + km) // PARTS
 
     def serve(i, q, static):
-        for k in (4, 3, 2, 1, 0):
+        for k in ORDER:
             back, rem = divmod(LAG[k] + PARTS - 1 - q, PARTS)
             if rem == 0:
                 guard(i >= back, functools.partial(stages[k], i - back))
@@ -195,7 +196,7 @@
             for cp in w_copies(1, 1):
                 cp.start()
         piece = jnp.dot(x_v[:, j * 1536 : (j + 1) * 1536], w_v[0, j * 1536 : (j + 1) * 1536], preferred_element_type=F32)
-        total = piece if total is None else total + piece
+        total = piece if total is None else piece + total
     pl.semaphore_wait(barrier, 3)
     finish(0, 0, total)
 
@@ -218,7 +219,7 @@
         total = None
         for q in range(PARTS):
             piece = jnp.dot(x_v[:, q * part_k : (q + 1) * part_k], w_v[slot, q * part_k : (q + 1) * part_k], preferred_element_type=F32)
-            total = piece if total is None else total + piece
+            total = piece if total is None else piece + total
             if q == PARTS - 1:
                 finish(i, slot, total)
             serve(i, q, static)

time: 142 us -> 139 us (0.979)
  Pallas kernels: 142 us -> 139 us
    pallas_call x1, Pallas kernels: 137 us -> 135 us  [device_step(): pl.pallas_call(functools.partial(kernel, n), out_shape=pltpu.VMEM((rows,...]
where the time goes in v6:
time: 139 us
  Pallas kernels  139 us (100%)
    pallas_call x1, Pallas kernels, device_step(): pl.pallas_call(functools.partial(kernel, n), out_shape=pltpu.VMEM((rows,...  135 us
    pallas_call x1, Pallas kernels, device_step(): pl.pallas_call(store, out_shape=jax.ShapeDtypeStruct((rows, cols), BF16),...  4.66 us

profile of v6, /device:TPU:0, one launch (start us, length us, event | category | flops | bytes accessed | tf_op | source)
XLA Modules:
  0.0 139.4 jit_solution(15445112343885300519)
XLA Ops:
  0.0 134.7 %shard_map.46.y_ref = bf16[512,12288]{1,0:T(8,128)(2,1)S(1)} custom-call(bf16[512,1536]{1,0:T(8,128)(2,1)} %ctx_ref.1, bf16[1536,12288]{1,0:T(8,128)(2,1)} %wo_ref.1, bf16[512,6144]{1,0:T(8,128)(2,1)} %act_ref.1, bf16[6144,12288]{1,0:T(8,128)(2,1)} %wd_ref.1), custom_call_target="tpu_custom_call" | custom-call | flops 96636764160 | bytes 188743680 | tf_op jit(solution)/shard_map/pallas_call | solution.py:263
  134.7 4.7 %shard_map.47 = bf16[512,12288]{1,0:T(8,128)(2,1)} custom-call(bf16[512,12288]{1,0:T(8,128)(2,1)S(1)} %shard_map.46.y_ref), custom_call_target="tpu_custom_call" | custom-call | bytes 12582912 | tf_op jit(solution)/shard_map/pallas_call | solution.py:288

commit v7 on v6

--- a/solution.py
+++ b/solution.py
@@ -12,14 +12,14 @@
 F32 = jnp.float32
 
 W = 512
-PARTS = 1
-LAG = (1, 3, 4, 5, 7)
+EARLY = 1280
+LAG = (0, 2, 3, 4, 6)
 ORDER = (1, 2, 3, 0, 4)
 HEAD = 1
 SLOTS = 4
 STORES = 8
 VMEM_LIMIT = 44 * 1024 * 1024
-DRAIN = ((4, 7), (0, 1), (1, 3), (2, 4), (3, 5), (4, 6), (1, 2), (1, 1), (2, 3), (3, 4), (4, 5), (2, 2), (2, 1), (3, 3), (4, 4), (3, 2), (3, 1), (4, 3), (4, 2), (4, 1))
+DRAIN = ((4, 6), (1, 2), (2, 3), (3, 4), (4, 5), (1, 1), (2, 2), (3, 3), (4, 4), (2, 1), (3, 2), (4, 3), (3, 1), (4, 2), (4, 1))
 
 
 def kernel(n_chunks, ctx_ref, wo_ref, act_ref, wd_ref, y_ref, x_v, w_v, recv0, recv1, recv2, send0, send1, send2, keep0, keep1, keep2, x_sem, w_sem, s_sem, r_sem):
@@ -174,17 +174,13 @@
         start(p5, c)
 
     stages = (stage0, stage1, stage2, stage3, stage4)
-    part_k = (ka + km) // PARTS
-
-    def serve(i, q, static):
+    def serve(i):
         for k in ORDER:
-            back, rem = divmod(LAG[k] + PARTS - 1 - q, PARTS)
-            if rem == 0:
-                guard(i >= back, functools.partial(stages[k], i - back))
-
-    def finish(i, slot, total):
-        send0[slot] = total[0:256].astype(BF16)
-        keep0[slot] = total[256:512]
+            back = LAG[k]
+            guard(i >= back, functools.partial(stages[k], i - back))
+
+    def push_out(i, slot, theirs):
+        send0[slot] = theirs.astype(BF16)
         for d in p0(i):
             d.start()
 
@@ -198,7 +194,9 @@
         piece = jnp.dot(x_v[:, j * 1536 : (j + 1) * 1536], w_v[0, j * 1536 : (j + 1) * 1536], preferred_element_type=F32)
         total = piece if total is None else piece + total
     pl.semaphore_wait(barrier, 3)
-    finish(0, 0, total)
+    push_out(0, 0, total[0:256])
+    keep0[0] = total[256:512]
+    serve(0)
 
     def step(i, static):
         slot = i % 2 if static else lax.rem(i, 2)
@@ -216,13 +214,11 @@
                 d.wait_send()
 
         guard(i >= 2, sent)
-        total = None
-        for q in range(PARTS):
-            piece = jnp.dot(x_v[:, q * part_k : (q + 1) * part_k], w_v[slot, q * part_k : (q + 1) * part_k], preferred_element_type=F32)
-            total = piece if total is None else piece + total
-            if q == PARTS - 1:
-                finish(i, slot, total)
-            serve(i, q, static)
+        theirs = jnp.dot(x_v[0:256], w_v[slot], preferred_element_type=F32)
+        early = jnp.dot(x_v[256:512, 0:EARLY], w_v[slot, 0:EARLY], preferred_element_type=F32)
+        push_out(i, slot, theirs)
+        keep0[slot] = jnp.dot(x_v[256:512, EARLY:], w_v[slot, EARLY:], preferred_element_type=F32) + early
+        serve(i)
 
     for i in range(1, HEAD):
         step(i, True)

time: 139 us -> 138 us (level)
    pallas_call x1, Pallas kernels: 135 us -> 133 us  [device_step(): pl.pallas_call(functools.partial(kernel, n), out_shape=pltpu.VMEM((rows,...]
where the time goes in v7:
time: 138 us
  Pallas kernels  138 us (100%)
    pallas_call x1, Pallas kernels, device_step(): pl.pallas_call(functools.partial(kernel, n), out_shape=pltpu.VMEM((rows,...  133 us
    pallas_call x1, Pallas kernels, device_step(): pl.pallas_call(store, out_shape=jax.ShapeDtypeStruct((rows, cols), BF16),...  4.66 us

profile of v7, /device:TPU:0, one launch (start us, length us, event | category | flops | bytes accessed | tf_op | source)
XLA Modules:
  0.0 137.6 jit_solution(1115417645984231635)
XLA Ops:
  0.0 132.9 %shard_map.46.y_ref = bf16[512,12288]{1,0:T(8,128)(2,1)S(1)} custom-call(bf16[512,1536]{1,0:T(8,128)(2,1)} %ctx_ref.1, bf16[1536,12288]{1,0:T(8,128)(2,1)} %wo_ref.1, bf16[512,6144]{1,0:T(8,128)(2,1)} %act_ref.1, bf16[6144,12288]{1,0:T(8,128)(2,1)} %wd_ref.1), custom_call_target="tpu_custom_call" | custom-call | flops 96636764160 | bytes 188743680 | tf_op jit(solution)/shard_map/pallas_call | solution.py:259
  133.0 4.7 %shard_map.47 = bf16[512,12288]{1,0:T(8,128)(2,1)} custom-call(bf16[512,12288]{1,0:T(8,128)(2,1)S(1)} %shard_map.46.y_ref), custom_call_target="tpu_custom_call" | custom-call | bytes 12582912 | tf_op jit(solution)/shard_map/pallas_call | solution.py:284

commit v8 on v7

--- a/solution.py
+++ b/solution.py
@@ -13,13 +13,13 @@
 
 W = 512
 EARLY = 1280
-LAG = (0, 2, 3, 4, 6)
-ORDER = (1, 2, 3, 0, 4)
+LAG = (0, 1, 2, 4, 6)
+ORDER = (0, 1, 3, 2, 4)
 HEAD = 1
 SLOTS = 4
 STORES = 8
 VMEM_LIMIT = 44 * 1024 * 1024
-DRAIN = ((4, 6), (1, 2), (2, 3), (3, 4), (4, 5), (1, 1), (2, 2), (3, 3), (4, 4), (2, 1), (3, 2), (4, 3), (3, 1), (4, 2), (4, 1))
+DRAIN = ((4, 6), (3, 4), (1, 1), (2, 2), (4, 5), (3, 3), (4, 4), (2, 1), (3, 2), (4, 3), (3, 1), (4, 2), (4, 1))
 
 
 def kernel(n_chunks, ctx_ref, wo_ref, act_ref, wd_ref, y_ref, x_v, w_v, recv0, recv1, recv2, send0, send1, send2, keep0, keep1, keep2, x_sem, w_sem, s_sem, r_sem):

time: 138 us -> 139 us (level)
  no operation moved by 1% of the time
where the time goes in v8:
time: 139 us; the launch traced here: 138 us
  Pallas kernels  138 us (99%)
    pallas_call x1, Pallas kernels, device_step(): pl.pallas_call(functools.partial(kernel, n), out_shape=pltpu.VMEM((rows,...  134 us
    pallas_call x1, Pallas kernels, device_step(): pl.pallas_call(store, out_shape=jax.ShapeDtypeStruct((rows, cols), BF16),...  4.66 us

profile of v8, /device:TPU:0, one launch (start us, length us, event | category | flops | bytes accessed | tf_op | source)
XLA Modules:
  0.0 138.5 jit_solution(17765851023464686385)
XLA Ops:
  0.0 133.8 %shard_map.46.y_ref = bf16[512,12288]{1,0:T(8,128)(2,1)S(1)} custom-call(bf16[512,1536]{1,0:T(8,128)(2,1)} %ctx_ref.1, bf16[1536,12288]{1,0:T(8,128)(2,1)} %wo_ref.1, bf16[512,6144]{1,0:T(8,128)(2,1)} %act_ref.1, bf16[6144,12288]{1,0:T(8,128)(2,1)} %wd_ref.1), custom_call_target="tpu_custom_call" | custom-call | flops 96636764160 | bytes 188743680 | tf_op jit(solution)/shard_map/pallas_call | solution.py:259
  133.8 4.7 %shard_map.47 = bf16[512,12288]{1,0:T(8,128)(2,1)} custom-call(bf16[512,12288]{1,0:T(8,128)(2,1)S(1)} %shard_map.46.y_ref), custom_call_target="tpu_custom_call" | custom-call | bytes 12582912 | tf_op jit(solution)/shard_map/pallas_call | solution.py:284

commit v9 on v8

--- a/solution.py
+++ b/solution.py
@@ -13,13 +13,13 @@
 
 W = 512
 EARLY = 1280
-LAG = (0, 1, 2, 4, 6)
-ORDER = (0, 1, 3, 2, 4)
+LAG = (0, 1, 3, 4, 6)
+ORDER = (0, 2, 1, 3, 4)
 HEAD = 1
 SLOTS = 4
 STORES = 8
 VMEM_LIMIT = 44 * 1024 * 1024
-DRAIN = ((4, 6), (3, 4), (1, 1), (2, 2), (4, 5), (3, 3), (4, 4), (2, 1), (3, 2), (4, 3), (3, 1), (4, 2), (4, 1))
+DRAIN = ((2, 3), (4, 6), (1, 1), (3, 4), (2, 2), (4, 5), (3, 3), (2, 1), (4, 4), (3, 2), (4, 3), (3, 1), (4, 2), (4, 1))
 
 
 def kernel(n_chunks, ctx_ref, wo_ref, act_ref, wd_ref, y_ref, x_v, w_v, recv0, recv1, recv2, send0, send1, send2, keep0, keep1, keep2, x_sem, w_sem, s_sem, r_sem):

time: 139 us -> 138 us (level)
  no operation moved by 1% of the time
where the time goes in v9:
time: 138 us
  Pallas kernels  138 us (100%)
    pallas_call x1, Pallas kernels, device_step(): pl.pallas_call(functools.partial(kernel, n), out_shape=pltpu.VMEM((rows,...  133 us
    pallas_call x1, Pallas kernels, device_step(): pl.pallas_call(store, out_shape=jax.ShapeDtypeStruct((rows, cols), BF16),...  4.66 us

profile of v9, /device:TPU:0, one launch (start us, length us, event | category | flops | bytes accessed | tf_op | source)
XLA Modules:
  0.0 138.0 jit_solution(213898242136437779)
XLA Ops:
  0.0 133.3 %shard_map.46.y_ref = bf16[512,12288]{1,0:T(8,128)(2,1)S(1)} custom-call(bf16[512,1536]{1,0:T(8,128)(2,1)} %ctx_ref.1, bf16[1536,12288]{1,0:T(8,128)(2,1)} %wo_ref.1, bf16[512,6144]{1,0:T(8,128)(2,1)} %act_ref.1, bf16[6144,12288]{1,0:T(8,128)(2,1)} %wd_ref.1), custom_call_target="tpu_custom_call" | custom-call | flops 96636764160 | bytes 188743680 | tf_op jit(solution)/shard_map/pallas_call | solution.py:259
  133.3 4.7 %shard_map.47 = bf16[512,12288]{1,0:T(8,128)(2,1)} custom-call(bf16[512,12288]{1,0:T(8,128)(2,1)S(1)} %shard_map.46.y_ref), custom_call_target="tpu_custom_call" | custom-call | bytes 12582912 | tf_op jit(solution)/shard_map/pallas_call | solution.py:284
